TPU v7x, 32 devices: a whole 2x2x4 slice. The times are simulated.
32 devices in a mesh: ka: 8 (over y, x, core), ga: 4 (over z).
Axes of the slice: x: 2, y: 2, z: 4, core: 2. Of those that a mesh axis runs over, the one named last changes fastest.
Arguments:
- psi: bfloat16 [8, 2, 128, 1024], P('ka', None, None, 'ga'), may hold values from -0.75 to 0.75
- dvscf: bfloat16 [96, 2, 1024], P(None, None, 'ga'), may hold values from -6 to 6
- kq_map: int32 [8], P('ka'), may hold values from 0 to 7, each once
Outputs:
- coupling: float32 [96, 8, 2, 128, 128], P('ga', 'ka')
Inputs may be any that keep to these rules, and one draw needn't show every extreme that they name: kq_map is a permutation of the k-points 0 to 7.
All inputs are finite; a program needn't handle non-finite values.
Results may differ from a plain program's by a relative error of at most 0.0029.
Values may be sent and summed in bfloat16 or wider, within the bound.
A program may use at most 128 MiB of HBM per device.

v0:
```python
import functools

import jax
import jax.numpy as jnp
from jax import lax
from jax.experimental import pallas as pl
from jax.experimental.pallas import tpu as pltpu
from jax.sharding import PartitionSpec as P

MESH = pl.DeviceIdType.MESH
BLOCK = 8


def kernel(
    kn, gn, psi_hbm, dv_hbm, kq_ref, out_ref,
    dv_ref, psi_near, psi_wide, phi_near, phi_wide, dv_all, dv_f32, kq_all,
    stage_near, stage_wide, choice_near, choice_wide, partial, prods,
    load, send_kq, send_one, send_two, send_psi, send_phi, send_stage, send_dv,
    recv_kq, recv_one, recv_two, recv_psi, recv_phi, recv_stage, recv_dv,
):
    ka = lax.axis_index("ka")
    ga = lax.axis_index("ga")
    rows, half = stage_near.shape[1], stage_near.shape[2]
    bands = kn * rows // 2
    modes = out_ref.shape[0]
    width = 2 if gn % 2 == 0 else 1

    def along_k(d):
        return lax.rem(ka + d, kn)

    def along_g(d):
        return lax.rem(ga + d, gn)

    first_half, second_half = pl.ds(0, half), pl.ds(half, half)
    loads = [
        pltpu.make_async_copy(psi_hbm.at[:, :, first_half], psi_near.at[ga], load.at[0]),
        pltpu.make_async_copy(psi_hbm.at[:, :, second_half], psi_wide.at[ga], load.at[1]),
        pltpu.make_async_copy(psi_hbm.at[ka, :, first_half], stage_near.at[ka], load.at[2]),
        pltpu.make_async_copy(psi_hbm.at[ka, :, second_half], stage_wide.at[ga, ka], load.at[3]),
        pltpu.make_async_copy(dv_hbm, dv_ref, load.at[4]),
    ]
    for c in loads:
        c.start()
    barrier = pltpu.get_barrier_semaphore()
    for d in range(1, gn):
        pl.semaphore_signal(barrier, inc=1, device_id=(ka, along_g(d)), device_id_type=MESH)
    for d in range(1, kn):
        pl.semaphore_signal(barrier, inc=1, device_id=(along_k(d), ga), device_id_type=MESH)
    for c in loads:
        c.wait()
    dv_all[ga] = dv_ref[ga]
    kq_all[ka] = kq_ref[...]
    pl.semaphore_wait(barrier, kn + gn - 2)

    def copy(src, dst, send, recv, to):
        return pltpu.make_async_remote_copy(
            src_ref=src, dst_ref=dst, send_sem=send, recv_sem=recv, device_id=to, device_id_type=MESH
        )

    def kq_copy(d, slot):
        return copy(kq_ref, kq_all.at[slot], send_kq.at[d], recv_kq.at[slot], (along_k(d), ga))

    def one_copies(d, slot):
        to = along_k(d)
        return (
            copy(psi_wide.at[ga, to], stage_wide.at[ga, slot], send_one.at[0, d], recv_one.at[0, slot], (to, ga)),
            copy(psi_near.at[ga, to], stage_near.at[slot], send_one.at[1, d], recv_one.at[1, slot], (to, ga)),
        )

    def own_copies(d, slot):
        to = along_k(d)
        return (
            copy(choice_near.at[to], phi_near.at[ga, slot], send_two.at[ga, 0, d], recv_two.at[ga, 0, slot], (to, ga)),
            copy(choice_wide.at[ga, to], phi_wide.at[ga, slot], send_two.at[ga, 1, d], recv_two.at[ga, 1, slot], (to, ga)),
        )

    def slab_copies(slab, d, slot):
        to = along_k(d)
        return (
            copy(stage_wide.at[slab, to], psi_wide.at[slab, slot], send_two.at[slab, 0, d], recv_two.at[slab, 0, slot], (to, ga)),
            copy(choice_wide.at[slab, to], phi_wide.at[slab, slot], send_two.at[slab, 1, d], recv_two.at[slab, 1, slot], (to, ga)),
        )

    def dv_copy(d, slot):
        return copy(dv_ref.at[along_g(d)], dv_all.at[slot], send_dv.at[d], recv_dv.at[slot], (ka, along_g(d)))

    def slab_copy(all_ref, send, recv, slab, to):
        return copy(all_ref.at[slab], all_ref.at[slab], send.at[to], recv.at[slab], (ka, to))

    def spread(copies):
        for hop in range(1, max(gn - 1, 2)):
            for to in (ga + hop, ga - hop):
                @pl.when((to >= 0) & (to < gn))
                def _():
                    copies(ga, to)

    def forward(copies):
        if gn > 2:
            @pl.when(ga == 1)
            def _():
                copies(gn - 1, 0)

            @pl.when(ga == gn - 2)
            def _():
                copies(0, gn - 1)

    def is_far(slab):
        if gn <= 2:
            return ga < 0
        return ((ga == 1) & (slab == gn - 1)) | ((ga == gn - 2) & (slab == 0))

    def slab_at(step):
        return ga ^ step if gn & (gn - 1) == 0 else along_g(step)

    psi_slab = functools.partial(slab_copy, psi_near, send_psi, recv_psi)
    phi_slab = functools.partial(slab_copy, phi_near, send_phi, recv_phi)
    stage_slab = functools.partial(slab_copy, stage_wide, send_stage, recv_stage)

    def pass_on(slabs, far, to):
        slabs(far, ga).wait_recv()
        slabs(far, to).start()

    def await_slab(slabs, slab):
        @pl.when(jnp.logical_not(is_far(slab)))
        def _():
            slabs(slab, ga).wait_recv()

    def choose(pieces, picks):
        def step(k, _):
            wanted = jnp.broadcast_to(kq_all[k], (rows, half))
            picked = jnp.zeros((rows, half), jnp.float32)
            for j in range(kn):
                picked = jnp.where(wanted == j, pieces[j].astype(jnp.float32), picked)
            picks[k] = picked.astype(jnp.bfloat16)
            return 0

        lax.fori_loop(0, kn, step, 0)

    def products(place, waves, side):
        slab = slab_at(place)
        lanes = slice(side * half, (side + 1) * half)
        start = place % width * 2 * half + side * half
        into = slice(start, start + half)
        if side == 0:
            dv_f32[slab] = dv_all[slab].astype(jnp.float32)

        def step(u, _):
            wave = waves[slab].reshape(2 * bands, half)
            wave_real = wave[:bands].astype(jnp.float32)
            wave_imag = wave[bands:].astype(jnp.float32)
            dv = dv_f32[slab, u]
            dv_real, dv_imag = dv[0:1, lanes], dv[1:2, lanes]
            prods[place // width, u, :bands, into] = (dv_real * wave_real - dv_imag * wave_imag).astype(jnp.bfloat16)
            prods[place // width, u, bands:, into] = (dv_real * wave_imag + dv_imag * wave_real).astype(jnp.bfloat16)
            return 0

        lax.fori_loop(0, modes, step, 0, unroll=2)

    for d in range(1, kn):
        kq_copy(d, ka).start()
        for c in one_copies(d, ka):
            c.start()
    spread(lambda slab, to: psi_slab(slab, to).start())
    products(0, psi_near, 0)
    products(0, psi_wide, 1)
    for d in range(1, kn):
        kq_copy(d, along_k(d)).wait_recv()
        for c in one_copies(d, along_k(d)):
            c.wait_recv()
    spread(lambda slab, to: stage_slab(slab, to).start())
    for d in range(1, gn):
        dv_copy(d, ga).start()

    choose(stage_near, choice_near)
    choose(stage_wide.at[ga], choice_wide.at[ga])
    for d in range(1, kn):
        for c in own_copies(d, ka):
            c.start()
    phi_near[ga, ka] = choice_near[ka]
    phi_wide[ga, ka] = choice_wide[ga, ka]
    forward(functools.partial(pass_on, psi_slab))
    for d in range(1, kn):
        for c in own_copies(d, along_k(d)):
            c.wait_recv()
    spread(lambda slab, to: phi_slab(slab, to).start())

    forward(functools.partial(pass_on, stage_slab))
    for step in range(1, gn):
        slab = slab_at(step)
        await_slab(stage_slab, slab)
        choose(stage_wide.at[slab], choice_wide.at[slab])
        for d in range(1, kn):
            for c in slab_copies(slab, d, ka):
                c.start()
        psi_wide[slab, ka] = stage_wide[slab, ka]
        phi_wide[slab, ka] = choice_wide[slab, ka]
        copy(dv_ref.at[0], dv_all.at[slab], send_dv.at[0], recv_dv.at[slab], (ka, ga)).wait_recv()
        await_slab(psi_slab, slab)
        products(step, psi_near, 0)

    block = BLOCK if modes % BLOCK == 0 else 1
    steps = modes // block
    for first in range(0, gn, width):
        slabs = [slab_at(first + i) for i in range(width)]
        last = first + width == gn
        if last and first == 0:
            forward(functools.partial(pass_on, phi_slab))
        for i, slab in enumerate(slabs):
            if first + i:
                for d in range(1, kn):
                    for c in slab_copies(slab, d, along_k(d)):
                        c.wait_recv()
                products(first + i, psi_wide, 1)
        for i, slab in enumerate(slabs):
            if first + i:
                if last:
                    await_slab(phi_slab, slab)
                else:
                    phi_slab(slab, ga).wait_recv()

        def mode_step(t, _):
            other = jnp.concatenate(
                [side[slab].reshape(2 * bands, half) for slab in slabs for side in (phi_near, phi_wide)], axis=1
            )
            full = lax.dot_general(
                prods[first // width, pl.ds(t * block, block)].reshape(block * 2 * bands, width * 2 * half),
                other, (((1,), (1,)), ((), ())), preferred_element_type=jnp.float32,
            )
            for q in range(block):
                u = t * block + q
                top, low = full[2 * q * bands:(2 * q + 1) * bands], full[(2 * q + 1) * bands:(2 * q + 2) * bands]
                real = top[:, :bands] + low[:, bands:]
                imag = low[:, :bands] - top[:, bands:]
                if first:
                    real = real + partial[u, 0]
                    imag = imag + partial[u, 1]
                if last:
                    out_ref[u, 0] = real.T
                    out_ref[u, 1] = imag.T
                else:
                    partial[u, 0] = real
                    partial[u, 1] = imag
            return 0

        if first == 0 and not last:
            lax.fori_loop(0, steps // 2, mode_step, 0)
            forward(functools.partial(pass_on, phi_slab))
            lax.fori_loop(steps // 2, steps, mode_step, 0)
        else:
            lax.fori_loop(0, steps, mode_step, 0)

    for d in range(1, kn):
        kq_copy(d, ka).wait_send()
        for c in one_copies(d, ka) + own_copies(d, ka):
            c.wait_send()
        for step in range(1, gn):
            for c in slab_copies(slab_at(step), d, ka):
                c.wait_send()
    for d in range(1, gn):
        dv_copy(d, ga).wait_send()
    for slabs in (psi_slab, phi_slab, stage_slab):
        spread(lambda own, to, slabs=slabs: slabs(own, to).wait_send())
        forward(lambda far, to, slabs=slabs: slabs(far, to).wait_send())


def body(psi, dvscf, kq_map):
    kn, gn = lax.axis_size("ka"), lax.axis_size("ga")
    _, parts, bands, cells = psi.shape
    rows = parts * bands // kn
    half = cells // 2
    modes = dvscf.shape[0] // gn
    pieces = pltpu.with_memory_space_constraint(psi.reshape(kn, rows, cells), pltpu.HBM)
    potential = pltpu.with_memory_space_constraint(dvscf.reshape(gn, modes, 2, cells), pltpu.HBM)
    wanted = jnp.broadcast_to(kq_map[:, None], (1, half)).astype(jnp.int32)
    width = 2 if gn % 2 == 0 else 1
    dma = pltpu.SemaphoreType.DMA
    bf16 = jnp.bfloat16
    out = pl.pallas_call(
        functools.partial(kernel, kn, gn),
        out_shape=jax.ShapeDtypeStruct((modes, 2, bands, bands), jnp.float32),
        in_specs=[
            pl.BlockSpec(memory_space=pltpu.HBM),
            pl.BlockSpec(memory_space=pltpu.HBM),
            pl.BlockSpec(memory_space=pltpu.VMEM),
        ],
        out_specs=pl.BlockSpec(memory_space=pltpu.VMEM),
        scratch_shapes=[
            pltpu.VMEM((gn, modes, 2, cells), bf16),
            pltpu.VMEM((gn, kn, rows, half), bf16),
            pltpu.VMEM((gn, kn, rows, half), bf16),
            pltpu.VMEM((gn, kn, rows, half), bf16),
            pltpu.VMEM((gn, kn, rows, half), bf16),
            pltpu.VMEM((gn, modes, 2, cells), bf16),
            pltpu.VMEM((gn, modes, 2, cells), jnp.float32),
            pltpu.VMEM((kn, 1, half), jnp.int32),
            pltpu.VMEM((kn, rows, half), bf16),
            pltpu.VMEM((gn, kn, rows, half), bf16),
            pltpu.VMEM((kn, rows, half), bf16),
            pltpu.VMEM((gn, kn, rows, half), bf16),
            pltpu.VMEM((modes, 2, bands, bands), jnp.float32),
            pltpu.VMEM((gn // width, modes, 2 * bands, width * cells), bf16),
            dma((5,)),
            dma((kn,)), dma((2, kn)), dma((gn, 2, kn)), dma((gn,)), dma((gn,)), dma((gn,)), dma((gn,)),
            dma((kn,)), dma((2, kn)), dma((gn, 2, kn)), dma((gn,)), dma((gn,)), dma((gn,)), dma((gn,)),
        ],
        compiler_params=pltpu.CompilerParams(collective_id=0, has_side_effects=True, vmem_limit_bytes=36 * 1024 * 1024),
    )(pieces, potential, wanted)
    return out[:, None]


def solution(mesh):
    return jax.shard_map(
        body,
        mesh=mesh,
        in_specs=(P("ka", None, None, "ga"), P(None, None, "ga"), P("ka")),
        out_specs=P("ga", "ka", None, None, None),
        check_vma=False,
    )
```

profile of v0, /device:TPU:0, one launch (start us, length us, event | category | flops | bytes accessed | tf_op | source)
XLA Modules:
  0.0 31.4 jit_solution(18046694396725561935)
XLA Ops:
  0.7 29.1 %shard_map.37 = f32[24,2,128,128]{3,2,1,0:T(8,128)S(1)} custom-call(bf16[8,32,256]{2,1,0:T(8,128)(2,1)} %bitcast.8, bf16[4,24,2,256]{3,2,1,0:T(2,128)(2,1)} %bitcast.9, s32[1,128]{1,0:T(1,128)S(1)} %broadcast_in_dim.12.kq_ref), custom_call_target="tpu_custom_call" | custom-call | tf_op jit(solution)/shard_map/pallas_call | solution.py:278
  29.7 1.7 %copy.7 = f32[24,1,2,128,128]{4,3,2,1,0:T(8,128)} copy(f32[24,1,2,128,128]{4,3,2,1,0:T(8,128)S(1)} %bitcast.7) | data formatting | bytes 6291456
  (1 shorter events, 0.0 us)
where the time goes:
time: 31.6 us; the launch traced here: 31.4 us
  Pallas kernels  29.1 us (92%)
  local copies, waits for them, and re-layouts  1.67 us (5%)
  between operations  0.67 us (2%)
    pallas_call x1, Pallas kernels, body(): pl.pallas_call(functools.partial(kernel, kn, gn), out_shape=jax.ShapeDtyp...  29.1 us
    unnamed x1, local copies, waits for them, and re-layouts  1.67 us

commit v1 on v0

v1 whole, which is shorter than its diff:
```python
import functools

import jax
import jax.numpy as jnp
from jax import lax
from jax.experimental import pallas as pl
from jax.experimental.pallas import tpu as pltpu
from jax.sharding import PartitionSpec as P

MESH = pl.DeviceIdType.MESH
BLOCK = 8


def slab_at(ga, gn, step):
    return ga ^ step if gn & (gn - 1) == 0 else lax.rem(ga + step, gn)


def pairs_of(gn):
    halves = [(0, 0), (0, 1)] + [(s, 1) for s in range(1, gn)] + [(s, 0) for s in range(1, gn)]
    return [halves[2 * c:2 * c + 2] for c in range(gn)]


def exchange(
    kn, gn, psi_hbm, dv_hbm, kq_ref, partial, tail_prods, phi_near,
    dv_ref, psi_near, psi_wide, phi_wide, dv_all, dv_f32, kq_all,
    stage_near, stage_wide, choice_near, choice_wide, prods,
    load, send_kq, send_one, send_own, send_slab, send_dv, send_psi, send_phi, send_stage,
    recv_kq, recv_one, recv_own, recv_slab, recv_dv, recv_psi, recv_phi, recv_stage,
):
    ka = lax.axis_index("ka")
    ga = lax.axis_index("ga")
    rows, half = stage_near.shape[1], stage_near.shape[2]
    bands = kn * rows // 2
    modes = partial.shape[0]
    others = pl.ds(0, kn - 1)

    def along_k(d):
        return lax.rem(ka + d, kn)

    def along_g(d):
        return lax.rem(ga + d, gn)

    first_half, second_half = pl.ds(0, half), pl.ds(half, half)
    loads = [
        pltpu.make_async_copy(psi_hbm.at[:, :, second_half], psi_wide.at[ga], load.at[0]),
        pltpu.make_async_copy(psi_hbm.at[:, :, first_half], psi_near.at[ga], load.at[1]),
        pltpu.make_async_copy(psi_hbm.at[ka, :, first_half], stage_near.at[ka], load.at[2]),
        pltpu.make_async_copy(psi_hbm.at[ka, :, second_half], stage_wide.at[ga, ka], load.at[3]),
        pltpu.make_async_copy(dv_hbm, dv_ref, load.at[4]),
    ]
    for c in loads:
        c.start()
    barrier = pltpu.get_barrier_semaphore()
    for d in range(1, gn):
        pl.semaphore_signal(barrier, inc=1, device_id=(ka, along_g(d)), device_id_type=MESH)
    for d in range(1, kn):
        pl.semaphore_signal(barrier, inc=1, device_id=(along_k(d), ga), device_id_type=MESH)
    for c in loads:
        c.wait()
    dv_all[ga] = dv_ref[ga]
    kq_all[ka] = kq_ref[...]
    pl.semaphore_wait(barrier, kn + gn - 2)

    def copy(src, dst, send, recv, to):
        return pltpu.make_async_remote_copy(
            src_ref=src, dst_ref=dst, send_sem=send, recv_sem=recv, device_id=to, device_id_type=MESH
        )

    def await_recv(ref, sem):
        copy(ref, ref, load.at[0], sem, (ka, ga)).wait_recv()

    def await_send(ref, sem):
        copy(ref, ref, sem, load.at[0], (ka, ga)).wait_send()

    def kq_start(d):
        copy(kq_ref, kq_all.at[ka], send_kq.at[0], recv_kq.at[0], (along_k(d), ga)).start()

    def one_start(side, d):
        to = along_k(d)
        if side:
            copy(psi_wide.at[ga, to], stage_wide.at[ga, ka], send_one.at[1], recv_one.at[1], (to, ga)).start()
        else:
            copy(psi_near.at[ga, to], stage_near.at[ka], send_one.at[0], recv_one.at[0], (to, ga)).start()

    def own_start(side, d):
        to = along_k(d)
        if side:
            copy(choice_wide.at[ga, to], phi_wide.at[ga, ka], send_own.at[1], recv_own.at[1], (to, ga)).start()
        else:
            copy(choice_near.at[to], phi_near.at[ga, ka], send_own.at[0], recv_own.at[0], (to, ga)).start()

    def slab_start(slab, d):
        to = along_k(d)
        copy(stage_wide.at[slab, to], psi_wide.at[slab, ka], send_slab.at[0], recv_slab.at[0, slab], (to, ga)).start()
        copy(choice_wide.at[slab, to], phi_wide.at[slab, ka], send_slab.at[1], recv_slab.at[1, slab], (to, ga)).start()

    def dv_start(d):
        copy(dv_ref.at[along_g(d)], dv_all.at[ga], send_dv.at[0], recv_dv.at[0], (ka, along_g(d))).start()

    def slab_copy(all_ref, send, recv, slab, to):
        return copy(all_ref.at[slab], all_ref.at[slab], send.at[to], recv.at[slab], (ka, to))

    def spread(copies):
        for hop in range(1, max(gn - 1, 2)):
            for to in (ga + hop, ga - hop):
                @pl.when((to >= 0) & (to < gn))
                def _():
                    copies(ga, to)

    def forward(copies):
        if gn > 2:
            @pl.when(ga == 1)
            def _():
                copies(gn - 1, 0)

            @pl.when(ga == gn - 2)
            def _():
                copies(0, gn - 1)

    def is_far(slab):
        if gn <= 2:
            return ga < 0
        return ((ga == 1) & (slab == gn - 1)) | ((ga == gn - 2) & (slab == 0))

    psi_slab = functools.partial(slab_copy, psi_near, send_psi, recv_psi)
    phi_slab = functools.partial(slab_copy, phi_near, send_phi, recv_phi)
    stage_slab = functools.partial(slab_copy, stage_wide, send_stage, recv_stage)

    def pass_on(slabs, far, to):
        slabs(far, ga).wait_recv()
        slabs(far, to).start()

    def await_slab(slabs, slab):
        @pl.when(jnp.logical_not(is_far(slab)))
        def _():
            slabs(slab, ga).wait_recv()

    def choose(pieces, picks):
        def step(k, _):
            wanted = jnp.broadcast_to(kq_all[k], (rows, half))
            picked = jnp.zeros((rows, half), jnp.float32)
            for j in range(kn):
                picked = jnp.where(wanted == j, pieces[j].astype(jnp.float32), picked)
            picks[k] = picked.astype(jnp.bfloat16)
            return 0

        lax.fori_loop(0, kn, step, 0)

    spots = {half_slab: (c, i) for c, pair in enumerate(pairs_of(gn)) for i, half_slab in enumerate(pair)}

    def products(place, side):
        slab = slab_at(ga, gn, place)
        waves = psi_wide if side else psi_near
        lanes = slice(side * half, (side + 1) * half)
        chunk, start = spots[place, side]
        into = slice(start * half, (start + 1) * half)
        target = tail_prods if chunk == gn - 1 else prods.at[chunk]

        def step(u, _):
            wave = waves[slab].reshape(2 * bands, half)
            wave_real = wave[:bands].astype(jnp.float32)
            wave_imag = wave[bands:].astype(jnp.float32)
            dv = dv_f32[slab, u]
            dv_real, dv_imag = dv[0:1, lanes], dv[1:2, lanes]
            target[u, :bands, into] = (dv_real * wave_real - dv_imag * wave_imag).astype(jnp.bfloat16)
            target[u, bands:, into] = (dv_real * wave_imag + dv_imag * wave_real).astype(jnp.bfloat16)
            return 0

        lax.fori_loop(0, modes, step, 0, unroll=2)

    def widen(slab):
        dv_f32[slab] = dv_all[slab].astype(jnp.float32)

    block = BLOCK if modes % BLOCK == 0 else 1

    def matmul(chunk):
        sides = [(phi_wide if side else phi_near, slab_at(ga, gn, place)) for place, side in pairs_of(gn)[chunk]]

        def mode_step(t, _):
            other = jnp.concatenate([ref[slab].reshape(2 * bands, half) for ref, slab in sides], axis=1)
            full = lax.dot_general(
                prods[chunk, pl.ds(t * block, block)].reshape(block * 2 * bands, 2 * half),
                other, (((1,), (1,)), ((), ())), preferred_element_type=jnp.float32,
            )
            for q in range(block):
                u = t * block + q
                top, low = full[2 * q * bands:(2 * q + 1) * bands], full[(2 * q + 1) * bands:(2 * q + 2) * bands]
                real = top[:, :bands] + low[:, bands:]
                imag = low[:, :bands] - top[:, bands:]
                if chunk:
                    real = real + partial[u, 0]
                    imag = imag + partial[u, 1]
                partial[u, 0] = real
                partial[u, 1] = imag
            return 0

        lax.fori_loop(0, modes // block, mode_step, 0)

    for d in range(1, kn):
        kq_start(d)
        one_start(1, d)
    for d in range(1, kn):
        one_start(0, d)
    spread(lambda slab, to: psi_slab(slab, to).start())
    widen(ga)
    products(0, 0)
    products(0, 1)
    await_recv(kq_all.at[others], recv_kq.at[0])
    await_recv(stage_wide.at[ga, others], recv_one.at[1])
    spread(lambda slab, to: stage_slab(slab, to).start())
    for d in range(1, gn):
        dv_start(d)
    await_recv(stage_near.at[others], recv_one.at[0])
    choose(stage_near, choice_near)
    for d in range(1, kn):
        own_start(0, d)
    choose(stage_wide.at[ga], choice_wide.at[ga])
    for d in range(1, kn):
        own_start(1, d)
    phi_near[ga, ka] = choice_near[ka]
    phi_wide[ga, ka] = choice_wide[ga, ka]
    forward(functools.partial(pass_on, psi_slab))
    await_recv(phi_near.at[ga, others], recv_own.at[0])
    spread(lambda slab, to: phi_slab(slab, to).start())

    forward(functools.partial(pass_on, stage_slab))
    await_recv(dv_all.at[pl.ds(0, gn - 1)], recv_dv.at[0])
    for step in range(1, gn):
        slab = slab_at(ga, gn, step)
        await_slab(stage_slab, slab)
        choose(stage_wide.at[slab], choice_wide.at[slab])
        for d in range(1, kn):
            slab_start(slab, d)
        psi_wide[slab, ka] = stage_wide[slab, ka]
        phi_wide[slab, ka] = choice_wide[slab, ka]
        widen(slab)
        await_slab(psi_slab, slab)
        products(step, 0)
    await_recv(phi_wide.at[ga, others], recv_own.at[1])
    matmul(0)
    forward(functools.partial(pass_on, phi_slab))
    for chunk in range(1, gn):
        for place, side in pairs_of(gn)[chunk]:
            slab = slab_at(ga, gn, place)
            if side:
                await_recv(psi_wide.at[slab, others], recv_slab.at[0, slab])
                await_recv(phi_wide.at[slab, others], recv_slab.at[1, slab])
                products(place, 1)
            else:
                await_slab(phi_slab, slab)
        if chunk < gn - 1:
            matmul(chunk)

    await_send(kq_all.at[others], send_kq.at[0])
    for side in range(2):
        await_send(stage_near.at[others], send_one.at[side])
        await_send(stage_near.at[others], send_own.at[side])
        await_send(stage_wide.at[pl.ds(0, gn - 1), others], send_slab.at[side])
    await_send(dv_ref.at[pl.ds(0, gn - 1)], send_dv.at[0])
    for slabs in (psi_slab, phi_slab, stage_slab):
        spread(lambda own, to, slabs=slabs: slabs(own, to).wait_send())
        forward(lambda far, to, slabs=slabs: slabs(far, to).wait_send())


def finish(gn, partial, prods, phi_near, out_hbm, out, done):
    ga = lax.axis_index("ga")
    modes, _, bands, _ = partial.shape
    half = phi_near.shape[3]
    slabs = [slab_at(ga, gn, place) for place, _ in pairs_of(gn)[gn - 1]]
    other = jnp.concatenate([phi_near[slab].reshape(2 * bands, half) for slab in slabs], axis=1)

    def mode_step(u, _):
        full = lax.dot_general(prods[u], other, (((1,), (1,)), ((), ())), preferred_element_type=jnp.float32)
        top, low = full[:bands], full[bands:]
        out[u, 0] = (partial[u, 0] + (top[:, :bands] + low[:, bands:])).T
        out[u, 1] = (partial[u, 1] + (low[:, :bands] - top[:, bands:])).T
        pltpu.make_async_copy(out.at[u], out_hbm.at[u], done).start()
        return 0

    lax.fori_loop(0, modes, mode_step, 0, unroll=24)
    pltpu.make_async_copy(out, out_hbm, done).wait()


def body(psi, dvscf, kq_map):
    kn, gn = lax.axis_size("ka"), lax.axis_size("ga")
    _, parts, bands, cells = psi.shape
    rows = parts * bands // kn
    half = cells // 2
    modes = dvscf.shape[0] // gn
    pieces = pltpu.with_memory_space_constraint(psi.reshape(kn, rows, cells), pltpu.HBM)
    potential = pltpu.with_memory_space_constraint(dvscf.reshape(gn, modes, 2, cells), pltpu.HBM)
    wanted = jnp.broadcast_to(kq_map[:, None], (1, half)).astype(jnp.int32)
    dma = pltpu.SemaphoreType.DMA
    bf16 = jnp.bfloat16
    in_hbm, in_vmem = pl.BlockSpec(memory_space=pltpu.HBM), pl.BlockSpec(memory_space=pltpu.VMEM)
    partial, prods, phi_near = pl.pallas_call(
        functools.partial(exchange, kn, gn),
        out_shape=[
            jax.ShapeDtypeStruct((modes, 2, bands, bands), jnp.float32),
            jax.ShapeDtypeStruct((modes, 2 * bands, cells), bf16),
            jax.ShapeDtypeStruct((gn, kn, rows, half), bf16),
        ],
        in_specs=[in_hbm, in_hbm, in_vmem],
        out_specs=[in_vmem] * 3,
        scratch_shapes=[
            pltpu.VMEM((gn, modes, 2, cells), bf16),
            pltpu.VMEM((gn, kn, rows, half), bf16),
            pltpu.VMEM((gn, kn, rows, half), bf16),
            pltpu.VMEM((gn, kn, rows, half), bf16),
            pltpu.VMEM((gn, modes, 2, cells), bf16),
            pltpu.VMEM((gn, modes, 2, cells), jnp.float32),
            pltpu.VMEM((kn, 1, half), jnp.int32),
            pltpu.VMEM((kn, rows, half), bf16),
            pltpu.VMEM((gn, kn, rows, half), bf16),
            pltpu.VMEM((kn, rows, half), bf16),
            pltpu.VMEM((gn, kn, rows, half), bf16),
            pltpu.VMEM((gn - 1, modes, 2 * bands, cells), bf16),
            dma((5,)),
            dma((1,)), dma((2,)), dma((2,)), dma((2,)), dma((1,)), dma((gn,)), dma((gn,)), dma((gn,)),
            dma((1,)), dma((2,)), dma((2,)), dma((2, gn)), dma((1,)), dma((gn,)), dma((gn,)), dma((gn,)),
        ],
        compiler_params=pltpu.CompilerParams(collective_id=0, has_side_effects=True, vmem_limit_bytes=40 * 1024 * 1024),
    )(pieces, potential, wanted)
    out = pl.pallas_call(
        functools.partial(finish, gn),
        out_shape=jax.ShapeDtypeStruct((modes, 2, bands, bands), jnp.float32),
        in_specs=[in_vmem] * 3,
        out_specs=in_hbm,
        scratch_shapes=[pltpu.VMEM((modes, 2, bands, bands), jnp.float32), dma],
        compiler_params=pltpu.CompilerParams(vmem_limit_bytes=16 * 1024 * 1024),
    )(partial, prods, phi_near)
    return out[:, None]


def solution(mesh):
    return jax.shard_map(
        body,
        mesh=mesh,
        in_specs=(P("ka", None, None, "ga"), P(None, None, "ga"), P("ka")),
        out_specs=P("ga", "ka", None, None, None),
        check_vma=False,
    )
```

time: 31.6 us -> 30.8 us (0.975)
  local copies, waits for them, and re-layouts: 1.67 us -> 0.01 us
  Pallas kernels: 29.1 us -> 30 us
    unnamed x1 -> x0, local copies, waits for them, and re-layouts: 1.67 us -> none
    pallas_call x1 -> x2, Pallas kernels: 29.1 us -> 30 us  [the longest x1 28 us: body(): pl.pallas_call(functools.partial(exchange, kn, gn), out_shape=[jax.ShapeD...]
where the time goes in v1:
time: 30.8 us; the launch traced here: 30.7 us
  Pallas kernels  30 us (97%)
  between operations  0.67 us (2%)
    pallas_call x1, Pallas kernels, body(): pl.pallas_call(functools.partial(exchange, kn, gn), out_shape=[jax.ShapeD...  28 us
    pallas_call x1, Pallas kernels, body(): pl.pallas_call(functools.partial(finish, gn), out_shape=jax.ShapeDtypeStr...  1.99 us

profile of v1, /device:TPU:0, one launch (start us, length us, event | category | flops | bytes accessed | tf_op | source)
XLA Modules:
  0.0 30.7 jit_solution(5676627197379749435)
XLA Ops:
  0.7 28.0 %shard_map.37 = (f32[24,2,128,128]{3,2,1,0:T(8,128)S(1)}, bf16[24,256,256]{2,1,0:T(8,128)(2,1)S(1)}, bf16[4,8,32,128]{3,2,1,0:T(8,128)(2,1)S(1)}) custom-call(bf16[8,32,256]{2,1,0:T(8,128)(2,1)} %bitcast.7, bf16[4,24,2,256]{3,2,1,0:T(2,128)(2,1)} %bitcast.8, s32[1,128]{1,0:T(1,128)S(1)} %broadcast_in_dim.12.kq_ref), custom_call_target="tpu_custom_call" | custom-call | tf_op jit(solution)/shard_map/pallas_call | solution.py:296
  28.7 2.0 %shard_map.38 = f32[24,2,128,128]{3,2,1,0:T(8,128)} custom-call(f32[24,2,128,128]{3,2,1,0:T(8,128)S(1)} %get-tuple-element.8.partial, bf16[24,256,256]{2,1,0:T(8,128)(2,1)S(1)} %get-tuple-element.9.prods, bf16[4,8,32,128]{3,2,1,0:T(8,128)(2,1)S(1)} %get-tuple-element.10.phi_near), custom_call_target="tpu_custom_call" | custom-call | tf_op jit(solution)/shard_map/pallas_call | solution.py:324
  (1 shorter events, 0.0 us)

commit v2 on v1

--- a/solution.py
+++ b/solution.py
@@ -9,10 +9,21 @@
 
 MESH = pl.DeviceIdType.MESH
 BLOCK = 8
+BAND_BLOCK = 32
+UNROLL = 24
+PSI = (False, False)
+STAGE = (False, False)
+PHI = (False, False)
 
 
 def slab_at(ga, gn, step):
-    return ga ^ step if gn & (gn - 1) == 0 else lax.rem(ga + step, gn)
+    if step == 0:
+        return ga
+    below, above = ga, gn - 1 - ga
+    both = jnp.minimum(below, above)
+    near = ga + (step + 1) // 2 if step % 2 else ga - step // 2
+    far = jnp.where(above > below, ga + (step - both), ga - (step - both))
+    return jnp.where(step <= 2 * both, near, far)
 
 
 def pairs_of(gn):
@@ -57,7 +68,6 @@
         pl.semaphore_signal(barrier, inc=1, device_id=(along_k(d), ga), device_id_type=MESH)
     for c in loads:
         c.wait()
-    dv_all[ga] = dv_ref[ga]
     kq_all[ka] = kq_ref[...]
     pl.semaphore_wait(barrier, kn + gn - 2)
 
@@ -94,21 +104,30 @@
         copy(stage_wide.at[slab, to], psi_wide.at[slab, ka], send_slab.at[0], recv_slab.at[0, slab], (to, ga)).start()
         copy(choice_wide.at[slab, to], phi_wide.at[slab, ka], send_slab.at[1], recv_slab.at[1, slab], (to, ga)).start()
 
+    shares, share = dv_all.shape[0], dv_all.shape[2]
+    own_share = ka if shares > 1 else 0
+
     def dv_start(d):
-        copy(dv_ref.at[along_g(d)], dv_all.at[ga], send_dv.at[0], recv_dv.at[0], (ka, along_g(d))).start()
+        piece = dv_ref.at[along_g(d), pl.ds(own_share * share, share)]
+        copy(piece, dv_all.at[own_share, ga], send_dv.at[0], recv_dv.at[0], (ka, along_g(d))).start()
+
+    def dv_share_start(d):
+        copy(dv_all.at[ka], dv_all.at[ka], send_dv.at[1], recv_dv.at[1], (along_k(d), ga)).start()
 
     def slab_copy(all_ref, send, recv, slab, to):
         return copy(all_ref.at[slab], all_ref.at[slab], send.at[to], recv.at[slab], (ka, to))
 
-    def spread(copies):
-        for hop in range(1, max(gn - 1, 2)):
+    def spread(slabs, act):
+        hops = range(1, gn) if slabs.direct else range(1, max(gn - 1, 2))
+        for hop in reversed(hops) if slabs.far_first else hops:
             for to in (ga + hop, ga - hop):
                 @pl.when((to >= 0) & (to < gn))
                 def _():
-                    copies(ga, to)
-
-    def forward(copies):
-        if gn > 2:
+                    act(slabs, ga, to)
+
+    def forward(slabs, act):
+        copies = functools.partial(act, slabs)
+        if gn > 2 and not slabs.direct:
             @pl.when(ga == 1)
             def _():
                 copies(gn - 1, 0)
@@ -125,15 +144,27 @@
     psi_slab = functools.partial(slab_copy, psi_near, send_psi, recv_psi)
     phi_slab = functools.partial(slab_copy, phi_near, send_phi, recv_phi)
     stage_slab = functools.partial(slab_copy, stage_wide, send_stage, recv_stage)
+    psi_slab.direct, psi_slab.far_first = PSI
+    phi_slab.direct, phi_slab.far_first = PHI
+    stage_slab.direct, stage_slab.far_first = STAGE
+
+    def start(slabs, slab, to):
+        slabs(slab, to).start()
+
+    def finish_send(slabs, slab, to):
+        slabs(slab, to).wait_send()
 
     def pass_on(slabs, far, to):
         slabs(far, ga).wait_recv()
         slabs(far, to).start()
 
     def await_slab(slabs, slab):
-        @pl.when(jnp.logical_not(is_far(slab)))
-        def _():
+        if slabs.direct:
             slabs(slab, ga).wait_recv()
+        else:
+            @pl.when(jnp.logical_not(is_far(slab)))
+            def _():
+                slabs(slab, ga).wait_recv()
 
     def choose(pieces, picks):
         def step(k, _):
@@ -156,20 +187,25 @@
         into = slice(start * half, (start + 1) * half)
         target = tail_prods if chunk == gn - 1 else prods.at[chunk]
 
-        def step(u, _):
-            wave = waves[slab].reshape(2 * bands, half)
-            wave_real = wave[:bands].astype(jnp.float32)
-            wave_imag = wave[bands:].astype(jnp.float32)
-            dv = dv_f32[slab, u]
-            dv_real, dv_imag = dv[0:1, lanes], dv[1:2, lanes]
-            target[u, :bands, into] = (dv_real * wave_real - dv_imag * wave_imag).astype(jnp.bfloat16)
-            target[u, bands:, into] = (dv_real * wave_imag + dv_imag * wave_real).astype(jnp.bfloat16)
-            return 0
-
-        lax.fori_loop(0, modes, step, 0, unroll=2)
+        wave = waves.at[slab]
+        span = min(BAND_BLOCK, rows)
+        for first in range(0, bands, span):
+            wave_real = wave[first // rows, first % rows:first % rows + span].astype(jnp.float32)
+            low = bands + first
+            wave_imag = wave[low // rows, low % rows:low % rows + span].astype(jnp.float32)
+
+            def step(u, _):
+                dv = dv_f32[slab, u]
+                dv_real, dv_imag = dv[0:1, lanes], dv[1:2, lanes]
+                target[u, first:first + span, into] = (dv_real * wave_real - dv_imag * wave_imag).astype(jnp.bfloat16)
+                target[u, low:low + span, into] = (dv_real * wave_imag + dv_imag * wave_real).astype(jnp.bfloat16)
+                return 0
+
+            lax.fori_loop(0, modes, step, 0, unroll=UNROLL)
 
     def widen(slab):
-        dv_f32[slab] = dv_all[slab].astype(jnp.float32)
+        for i in range(shares):
+            dv_f32[slab, i * share:(i + 1) * share] = dv_all[i, slab].astype(jnp.float32)
 
     block = BLOCK if modes % BLOCK == 0 else 1
 
@@ -194,38 +230,42 @@
                 partial[u, 1] = imag
             return 0
 
-        lax.fori_loop(0, modes // block, mode_step, 0)
+        lax.fori_loop(0, modes // block, mode_step, 0, unroll=True)
 
     for d in range(1, kn):
         kq_start(d)
         one_start(1, d)
+    for d in range(1, gn):
+        dv_start(d)
     for d in range(1, kn):
         one_start(0, d)
-    spread(lambda slab, to: psi_slab(slab, to).start())
-    widen(ga)
+    spread(psi_slab, start)
+    dv_f32[ga] = dv_ref[ga].astype(jnp.float32)
     products(0, 0)
     products(0, 1)
     await_recv(kq_all.at[others], recv_kq.at[0])
     await_recv(stage_wide.at[ga, others], recv_one.at[1])
-    spread(lambda slab, to: stage_slab(slab, to).start())
-    for d in range(1, gn):
-        dv_start(d)
+    spread(stage_slab, start)
     await_recv(stage_near.at[others], recv_one.at[0])
     choose(stage_near, choice_near)
     for d in range(1, kn):
         own_start(0, d)
+    await_recv(dv_all.at[0, pl.ds(0, gn - 1)], recv_dv.at[0])
+    if shares > 1:
+        for d in range(1, kn):
+            dv_share_start(d)
     choose(stage_wide.at[ga], choice_wide.at[ga])
     for d in range(1, kn):
         own_start(1, d)
     phi_near[ga, ka] = choice_near[ka]
     phi_wide[ga, ka] = choice_wide[ga, ka]
-    forward(functools.partial(pass_on, psi_slab))
+    forward(psi_slab, pass_on)
     await_recv(phi_near.at[ga, others], recv_own.at[0])
-    spread(lambda slab, to: phi_slab(slab, to).start())
-
-    forward(functools.partial(pass_on, stage_slab))
-    await_recv(dv_all.at[pl.ds(0, gn - 1)], recv_dv.at[0])
-    for step in range(1, gn):
+    spread(phi_slab, start)
+    if shares > 1:
+        await_recv(dv_all.at[others], recv_dv.at[1])
+
+    def relay_step(step):
         slab = slab_at(ga, gn, step)
         await_slab(stage_slab, slab)
         choose(stage_wide.at[slab], choice_wide.at[slab])
@@ -233,12 +273,20 @@
             slab_start(slab, d)
         psi_wide[slab, ka] = stage_wide[slab, ka]
         phi_wide[slab, ka] = choice_wide[slab, ka]
+
+    def near_step(step):
+        slab = slab_at(ga, gn, step)
         widen(slab)
         await_slab(psi_slab, slab)
         products(step, 0)
+
+    forward(stage_slab, pass_on)
+    for step in range(1, gn):
+        relay_step(step)
+        near_step(step)
     await_recv(phi_wide.at[ga, others], recv_own.at[1])
     matmul(0)
-    forward(functools.partial(pass_on, phi_slab))
+    forward(phi_slab, pass_on)
     for chunk in range(1, gn):
         for place, side in pairs_of(gn)[chunk]:
             slab = slab_at(ga, gn, place)
@@ -256,10 +304,12 @@
         await_send(stage_near.at[others], send_one.at[side])
         await_send(stage_near.at[others], send_own.at[side])
         await_send(stage_wide.at[pl.ds(0, gn - 1), others], send_slab.at[side])
-    await_send(dv_ref.at[pl.ds(0, gn - 1)], send_dv.at[0])
+    await_send(dv_all.at[0, pl.ds(0, gn - 1)], send_dv.at[0])
+    if shares > 1:
+        await_send(dv_all.at[others], send_dv.at[1])
     for slabs in (psi_slab, phi_slab, stage_slab):
-        spread(lambda own, to, slabs=slabs: slabs(own, to).wait_send())
-        forward(lambda far, to, slabs=slabs: slabs(far, to).wait_send())
+        spread(slabs, finish_send)
+        forward(slabs, finish_send)
 
 
 def finish(gn, partial, prods, phi_near, out_hbm, out, done):
@@ -287,6 +337,7 @@
     rows = parts * bands // kn
     half = cells // 2
     modes = dvscf.shape[0] // gn
+    shares = kn if modes % kn == 0 else 1
     pieces = pltpu.with_memory_space_constraint(psi.reshape(kn, rows, cells), pltpu.HBM)
     potential = pltpu.with_memory_space_constraint(dvscf.reshape(gn, modes, 2, cells), pltpu.HBM)
     wanted = jnp.broadcast_to(kq_map[:, None], (1, half)).astype(jnp.int32)
@@ -307,7 +358,7 @@
             pltpu.VMEM((gn, kn, rows, half), bf16),
             pltpu.VMEM((gn, kn, rows, half), bf16),
             pltpu.VMEM((gn, kn, rows, half), bf16),
-            pltpu.VMEM((gn, modes, 2, cells), bf16),
+            pltpu.VMEM((shares, gn, modes // shares, 2, cells), bf16),
             pltpu.VMEM((gn, modes, 2, cells), jnp.float32),
             pltpu.VMEM((kn, 1, half), jnp.int32),
             pltpu.VMEM((kn, rows, half), bf16),
@@ -316,8 +367,8 @@
             pltpu.VMEM((gn, kn, rows, half), bf16),
             pltpu.VMEM((gn - 1, modes, 2 * bands, cells), bf16),
             dma((5,)),
-            dma((1,)), dma((2,)), dma((2,)), dma((2,)), dma((1,)), dma((gn,)), dma((gn,)), dma((gn,)),
-            dma((1,)), dma((2,)), dma((2,)), dma((2, gn)), dma((1,)), dma((gn,)), dma((gn,)), dma((gn,)),
+            dma((1,)), dma((2,)), dma((2,)), dma((2,)), dma((2,)), dma((gn,)), dma((gn,)), dma((gn,)),
+            dma((1,)), dma((2,)), dma((2,)), dma((2, gn)), dma((2,)), dma((gn,)), dma((gn,)), dma((gn,)),
         ],
         compiler_params=pltpu.CompilerParams(collective_id=0, has_side_effects=True, vmem_limit_bytes=40 * 1024 * 1024),
     )(pieces, potential, wanted)

time: 30.8 us -> 27.8 us (0.903)
  Pallas kernels: 30 us -> 26.9 us
    pallas_call x1, Pallas kernels: 28 us -> 24.9 us  [body(): pl.pallas_call(functools.partial(exchange, kn, gn), out_shape=[jax.ShapeD...]
where the time goes in v2:
time: 27.8 us; the launch traced here: 27.6 us
  Pallas kernels  26.9 us (97%)
  between operations  0.67 us (2%)
    pallas_call x1, Pallas kernels, body(): pl.pallas_call(functools.partial(exchange, kn, gn), out_shape=[jax.ShapeD...  24.9 us
    pallas_call x1, Pallas kernels, body(): pl.pallas_call(functools.partial(finish, gn), out_shape=jax.ShapeDtypeStr...  2 us

profile of v2, /device:TPU:0, one launch (start us, length us, event | category | flops | bytes accessed | tf_op | source)
XLA Modules:
  0.0 27.6 jit_solution(5662643178603795395)
XLA Ops:
  0.7 24.9 %shard_map.37 = (f32[24,2,128,128]{3,2,1,0:T(8,128)S(1)}, bf16[24,256,256]{2,1,0:T(8,128)(2,1)S(1)}, bf16[4,8,32,128]{3,2,1,0:T(8,128)(2,1)S(1)}) custom-call(bf16[8,32,256]{2,1,0:T(8,128)(2,1)} %bitcast.7, bf16[4,24,2,256]{3,2,1,0:T(2,128)(2,1)} %bitcast.8, s32[1,128]{1,0:T(1,128)S(1)} %broadcast_in_dim.12.kq_ref), custom_call_target="tpu_custom_call" | custom-call | tf_op jit(solution)/shard_map/pallas_call | solution.py:347
  25.6 2.0 %shard_map.38 = f32[24,2,128,128]{3,2,1,0:T(8,128)} custom-call(f32[24,2,128,128]{3,2,1,0:T(8,128)S(1)} %get-tuple-element.8.partial, bf16[24,256,256]{2,1,0:T(8,128)(2,1)S(1)} %get-tuple-element.9.prods, bf16[4,8,32,128]{3,2,1,0:T(8,128)(2,1)S(1)} %get-tuple-element.10.phi_near), custom_call_target="tpu_custom_call" | custom-call | tf_op jit(solution)/shard_map/pallas_call | solution.py:375
  (1 shorter events, 0.0 us)

commit v3 on v2

--- a/solution.py
+++ b/solution.py
@@ -209,10 +209,32 @@
 
     block = BLOCK if modes % BLOCK == 0 else 1
 
-    def matmul(chunk):
+    def block_products(place, side, first_mode):
+        slab = slab_at(ga, gn, place)
+        wave = (psi_wide if side else psi_near).at[slab]
+        lanes = slice(side * half, (side + 1) * half)
+        chunk, start = spots[place, side]
+        into = slice(start * half, (start + 1) * half)
+        span = min(BAND_BLOCK, rows)
+        for first in range(0, bands, span):
+            low = bands + first
+            wave_real = wave[first // rows, first % rows:first % rows + span].astype(jnp.float32)
+            wave_imag = wave[low // rows, low % rows:low % rows + span].astype(jnp.float32)
+            for q in range(block):
+                dv = dv_f32[slab, first_mode + q]
+                dv_real, dv_imag = dv[0:1, lanes], dv[1:2, lanes]
+                u = first_mode + q
+                real = (dv_real * wave_real - dv_imag * wave_imag).astype(jnp.bfloat16)
+                imag = (dv_real * wave_imag + dv_imag * wave_real).astype(jnp.bfloat16)
+                prods[chunk, u, first:first + span, into] = real
+                prods[chunk, u, low:low + span, into] = imag
+
+    def matmul(chunk, fresh=()):
         sides = [(phi_wide if side else phi_near, slab_at(ga, gn, place)) for place, side in pairs_of(gn)[chunk]]
 
         def mode_step(t, _):
+            for place, side in fresh:
+                block_products(place, side, t * block)
             other = jnp.concatenate([ref[slab].reshape(2 * bands, half) for ref, slab in sides], axis=1)
             full = lax.dot_general(
                 prods[chunk, pl.ds(t * block, block)].reshape(block * 2 * bands, 2 * half),
@@ -281,23 +303,28 @@
         products(step, 0)
 
     forward(stage_slab, pass_on)
+    await_recv(phi_wide.at[ga, others], recv_own.at[1])
     for step in range(1, gn):
         relay_step(step)
+        if step == 1:
+            matmul(0)
+        if step == gn - 2:
+            near_step(1)
+    forward(phi_slab, pass_on)
+    for step in range(2, gn):
         near_step(step)
-    await_recv(phi_wide.at[ga, others], recv_own.at[1])
-    matmul(0)
-    forward(phi_slab, pass_on)
     for chunk in range(1, gn):
         for place, side in pairs_of(gn)[chunk]:
             slab = slab_at(ga, gn, place)
             if side:
                 await_recv(psi_wide.at[slab, others], recv_slab.at[0, slab])
                 await_recv(phi_wide.at[slab, others], recv_slab.at[1, slab])
-                products(place, 1)
+                if chunk == gn - 1:
+                    products(place, 1)
             else:
                 await_slab(phi_slab, slab)
         if chunk < gn - 1:
-            matmul(chunk)
+            matmul(chunk, [(place, side) for place, side in pairs_of(gn)[chunk] if side])
 
     await_send(kq_all.at[others], send_kq.at[0])
     for side in range(2):

time: 27.8 us -> 26.9 us (0.968)
  Pallas kernels: 26.9 us -> 26 us
    pallas_call x1, Pallas kernels: 24.9 us -> 24 us  [body(): pl.pallas_call(functools.partial(exchange, kn, gn), out_shape=[jax.ShapeD...]
where the time goes in v3:
time: 26.9 us; the launch traced here: 26.7 us
  Pallas kernels  26 us (97%)
  between operations  0.67 us (2%)
    pallas_call x1, Pallas kernels, body(): pl.pallas_call(functools.partial(exchange, kn, gn), out_shape=[jax.ShapeD...  24 us
    pallas_call x1, Pallas kernels, body(): pl.pallas_call(functools.partial(finish, gn), out_shape=jax.ShapeDtypeStr...  2 us

profile of v3, /device:TPU:0, one launch (start us, length us, event | category | flops | bytes accessed | tf_op | source)
XLA Modules:
  0.0 26.7 jit_solution(6200224916967049410)
XLA Ops:
  0.7 24.0 %shard_map.37 = (f32[24,2,128,128]{3,2,1,0:T(8,128)S(1)}, bf16[24,256,256]{2,1,0:T(8,128)(2,1)S(1)}, bf16[4,8,32,128]{3,2,1,0:T(8,128)(2,1)S(1)}) custom-call(bf16[8,32,256]{2,1,0:T(8,128)(2,1)} %bitcast.7, bf16[4,24,2,256]{3,2,1,0:T(2,128)(2,1)} %bitcast.8, s32[1,128]{1,0:T(1,128)S(1)} %broadcast_in_dim.12.kq_ref), custom_call_target="tpu_custom_call" | custom-call | tf_op jit(solution)/shard_map/pallas_call | solution.py:374
  24.7 2.0 %shard_map.38 = f32[24,2,128,128]{3,2,1,0:T(8,128)} custom-call(f32[24,2,128,128]{3,2,1,0:T(8,128)S(1)} %get-tuple-element.8.partial, bf16[24,256,256]{2,1,0:T(8,128)(2,1)S(1)} %get-tuple-element.9.prods, bf16[4,8,32,128]{3,2,1,0:T(8,128)(2,1)S(1)} %get-tuple-element.10.phi_near), custom_call_target="tpu_custom_call" | custom-call | tf_op jit(solution)/shard_map/pallas_call | solution.py:402
  (1 shorter events, 0.0 us)

commit v4 on v3

--- a/solution.py
+++ b/solution.py
@@ -27,14 +27,15 @@
 
 
 def pairs_of(gn):
-    halves = [(0, 0), (0, 1)] + [(s, 1) for s in range(1, gn)] + [(s, 0) for s in range(1, gn)]
+    last = gn - 1
+    halves = [(0, 0), (0, 1)] + [(s, side) for side in (1, 0) for s in range(1, last)] + [(last, 1), (last, 0)]
     return [halves[2 * c:2 * c + 2] for c in range(gn)]
 
 
 def exchange(
-    kn, gn, psi_hbm, dv_hbm, kq_ref, partial, tail_prods, phi_near,
-    dv_ref, psi_near, psi_wide, phi_wide, dv_all, dv_f32, kq_all,
-    stage_near, stage_wide, choice_near, choice_wide, prods,
+    kn, gn, psi_hbm, dv_hbm, kq_ref, partial, tail_prods, phi_near, phi_wide,
+    dv_ref, psi_near, psi_wide, dv_all, dv_f32, kq_all,
+    stage_near, stage_wide, choice_near, choice_wide, table, prods,
     load, send_kq, send_one, send_own, send_slab, send_dv, send_psi, send_phi, send_stage,
     recv_kq, recv_one, recv_own, recv_slab, recv_dv, recv_psi, recv_phi, recv_stage,
 ):
@@ -166,16 +167,12 @@
             def _():
                 slabs(slab, ga).wait_recv()
 
+    wanted = []
+
     def choose(pieces, picks):
-        def step(k, _):
-            wanted = jnp.broadcast_to(kq_all[k], (rows, half))
-            picked = jnp.zeros((rows, half), jnp.float32)
-            for j in range(kn):
-                picked = jnp.where(wanted == j, pieces[j].astype(jnp.float32), picked)
-            picks[k] = picked.astype(jnp.bfloat16)
-            return 0
-
-        lax.fori_loop(0, kn, step, 0)
+        table[...] = pieces[...]
+        for k in range(kn):
+            picks[k] = table[wanted[k]]
 
     spots = {half_slab: (c, i) for c, pair in enumerate(pairs_of(gn)) for i, half_slab in enumerate(pair)}
 
@@ -266,6 +263,8 @@
     products(0, 0)
     products(0, 1)
     await_recv(kq_all.at[others], recv_kq.at[0])
+    for k in range(kn):
+        wanted.append(jnp.max(kq_all[k]))
     await_recv(stage_wide.at[ga, others], recv_one.at[1])
     spread(stage_slab, start)
     await_recv(stage_near.at[others], recv_one.at[0])
@@ -308,11 +307,10 @@
         relay_step(step)
         if step == 1:
             matmul(0)
-        if step == gn - 2:
-            near_step(1)
+        if step < gn - 1:
+            near_step(step)
     forward(phi_slab, pass_on)
-    for step in range(2, gn):
-        near_step(step)
+    near_step(gn - 1)
     for chunk in range(1, gn):
         for place, side in pairs_of(gn)[chunk]:
             slab = slab_at(ga, gn, place)
@@ -339,12 +337,12 @@
         forward(slabs, finish_send)
 
 
-def finish(gn, partial, prods, phi_near, out_hbm, out, done):
+def finish(gn, partial, prods, phi_near, phi_wide, out_hbm, out, done):
     ga = lax.axis_index("ga")
     modes, _, bands, _ = partial.shape
     half = phi_near.shape[3]
-    slabs = [slab_at(ga, gn, place) for place, _ in pairs_of(gn)[gn - 1]]
-    other = jnp.concatenate([phi_near[slab].reshape(2 * bands, half) for slab in slabs], axis=1)
+    sides = [(phi_wide if side else phi_near, slab_at(ga, gn, place)) for place, side in pairs_of(gn)[gn - 1]]
+    other = jnp.concatenate([ref[slab].reshape(2 * bands, half) for ref, slab in sides], axis=1)
 
     def mode_step(u, _):
         full = lax.dot_general(prods[u], other, (((1,), (1,)), ((), ())), preferred_element_type=jnp.float32)
@@ -371,18 +369,18 @@
     dma = pltpu.SemaphoreType.DMA
     bf16 = jnp.bfloat16
     in_hbm, in_vmem = pl.BlockSpec(memory_space=pltpu.HBM), pl.BlockSpec(memory_space=pltpu.VMEM)
-    partial, prods, phi_near = pl.pallas_call(
+    partial, prods, phi_near, phi_wide = pl.pallas_call(
         functools.partial(exchange, kn, gn),
         out_shape=[
             jax.ShapeDtypeStruct((modes, 2, bands, bands), jnp.float32),
             jax.ShapeDtypeStruct((modes, 2 * bands, cells), bf16),
             jax.ShapeDtypeStruct((gn, kn, rows, half), bf16),
+            jax.ShapeDtypeStruct((gn, kn, rows, half), bf16),
         ],
         in_specs=[in_hbm, in_hbm, in_vmem],
-        out_specs=[in_vmem] * 3,
+        out_specs=[in_vmem] * 4,
         scratch_shapes=[
             pltpu.VMEM((gn, modes, 2, cells), bf16),
-            pltpu.VMEM((gn, kn, rows, half), bf16),
             pltpu.VMEM((gn, kn, rows, half), bf16),
             pltpu.VMEM((gn, kn, rows, half), bf16),
             pltpu.VMEM((shares, gn, modes // shares, 2, cells), bf16),
@@ -392,6 +390,7 @@
             pltpu.VMEM((gn, kn, rows, half), bf16),
             pltpu.VMEM((kn, rows, half), bf16),
             pltpu.VMEM((gn, kn, rows, half), bf16),
+            pltpu.VMEM((kn, rows, half), bf16),
             pltpu.VMEM((gn - 1, modes, 2 * bands, cells), bf16),
             dma((5,)),
             dma((1,)), dma((2,)), dma((2,)), dma((2,)), dma((2,)), dma((gn,)), dma((gn,)), dma((gn,)),
@@ -402,11 +401,11 @@
     out = pl.pallas_call(
         functools.partial(finish, gn),
         out_shape=jax.ShapeDtypeStruct((modes, 2, bands, bands), jnp.float32),
-        in_specs=[in_vmem] * 3,
+        in_specs=[in_vmem] * 4,
         out_specs=in_hbm,
         scratch_shapes=[pltpu.VMEM((modes, 2, bands, bands), jnp.float32), dma],
         compiler_params=pltpu.CompilerParams(vmem_limit_bytes=16 * 1024 * 1024),
-    )(partial, prods, phi_near)
+    )(partial, prods, phi_near, phi_wide)
     return out[:, None]
 
 

time: 26.9 us -> 26.3 us (0.978)
  Pallas kernels: 26 us -> 25.5 us
    pallas_call x1, Pallas kernels: 24 us -> 23.5 us  [body(): pl.pallas_call(functools.partial(exchange, kn, gn), out_shape=[jax.ShapeD...]
where the time goes in v4:
time: 26.3 us; the launch traced here: 26.2 us
  Pallas kernels  25.5 us (97%)
  between operations  0.67 us (3%)
    pallas_call x1, Pallas kernels, body(): pl.pallas_call(functools.partial(exchange, kn, gn), out_shape=[jax.ShapeD...  23.5 us
    pallas_call x1, Pallas kernels, body(): pl.pallas_call(functools.partial(finish, gn), out_shape=jax.ShapeDtypeStr...  1.99 us

profile of v4, /device:TPU:0, one launch (start us, length us, event | category | flops | bytes accessed | tf_op | source)
XLA Modules:
  0.0 26.2 jit_solution(124427144514666716)
XLA Ops:
  0.7 23.5 %shard_map.37 = (f32[24,2,128,128]{3,2,1,0:T(8,128)S(1)}, bf16[24,256,256]{2,1,0:T(8,128)(2,1)S(1)}, bf16[4,8,32,128]{3,2,1,0:T(8,128)(2,1)S(1)}, bf16[4,8,32,128]{3,2,1,0:T(8,128)(2,1)S(1)}) custom-call(bf16[8,32,256]{2,1,0:T(8,128)(2,1)} %bitcast.7, bf16[4,24,2,256]{3,2,1,0:T(2,128)(2,1)} %bitcast.8, s32[1,128]{1,0:T(1,128)S(1)} %broadcast_in_dim.12.kq_ref), custom_call_target="tpu_custom_call" | custom-call | tf_op jit(solution)/shard_map/pallas_call | solution.py:372
  24.2 2.0 %shard_map.38 = f32[24,2,128,128]{3,2,1,0:T(8,128)} custom-call(f32[24,2,128,128]{3,2,1,0:T(8,128)S(1)} %get-tuple-element.9.partial, bf16[24,256,256]{2,1,0:T(8,128)(2,1)S(1)} %get-tuple-element.10.prods, bf16[4,8,32,128]{3,2,1,0:T(8,128)(2,1)S(1)} %get-tuple-element.11.phi_near, bf16[4,8,32,128]{3,2,1,0:T(8,128)(2,1)S(1)} %get-tuple-element.12.phi_wide), custom_call_target="tpu_custom_call" | custom-call | tf_op jit(solution)/shard_map/pallas_call | solution.py:401
  (1 shorter events, 0.0 us)

commit v5 on v4

--- a/solution.py
+++ b/solution.py
@@ -11,8 +11,8 @@
 BLOCK = 8
 BAND_BLOCK = 32
 UNROLL = 24
-PSI = (False, False)
-STAGE = (False, False)
+PSI = (False, True)
+STAGE = (False, True)
 PHI = (False, False)
 
 

time: 26.3 us -> 26.3 us (level)
  no operation moved by 1% of the time
where the time goes in v5:
time: 26.3 us; the launch traced here: 26.1 us
  Pallas kernels  25.4 us (97%)
  between operations  0.67 us (3%)
    pallas_call x1, Pallas kernels, body(): pl.pallas_call(functools.partial(exchange, kn, gn), out_shape=[jax.ShapeD...  23.4 us
    pallas_call x1, Pallas kernels, body(): pl.pallas_call(functools.partial(finish, gn), out_shape=jax.ShapeDtypeStr...  2 us

profile of v5, /device:TPU:0, one launch (start us, length us, event | category | flops | bytes accessed | tf_op | source)
XLA Modules:
  0.0 26.1 jit_solution(17944881386563181703)
XLA Ops:
  0.7 23.4 %shard_map.37 = (f32[24,2,128,128]{3,2,1,0:T(8,128)S(1)}, bf16[24,256,256]{2,1,0:T(8,128)(2,1)S(1)}, bf16[4,8,32,128]{3,2,1,0:T(8,128)(2,1)S(1)}, bf16[4,8,32,128]{3,2,1,0:T(8,128)(2,1)S(1)}) custom-call(bf16[8,32,256]{2,1,0:T(8,128)(2,1)} %bitcast.7, bf16[4,24,2,256]{3,2,1,0:T(2,128)(2,1)} %bitcast.8, s32[1,128]{1,0:T(1,128)S(1)} %broadcast_in_dim.12.kq_ref), custom_call_target="tpu_custom_call" | custom-call | tf_op jit(solution)/shard_map/pallas_call | solution.py:372
  24.1 2.0 %shard_map.38 = f32[24,2,128,128]{3,2,1,0:T(8,128)} custom-call(f32[24,2,128,128]{3,2,1,0:T(8,128)S(1)} %get-tuple-element.9.partial, bf16[24,256,256]{2,1,0:T(8,128)(2,1)S(1)} %get-tuple-element.10.prods, bf16[4,8,32,128]{3,2,1,0:T(8,128)(2,1)S(1)} %get-tuple-element.11.phi_near, bf16[4,8,32,128]{3,2,1,0:T(8,128)(2,1)S(1)} %get-tuple-element.12.phi_wide), custom_call_target="tpu_custom_call" | custom-call | tf_op jit(solution)/shard_map/pallas_call | solution.py:401
  (1 shorter events, 0.0 us)
